TPU v7x, 32 devices: a whole 2x2x4 slice. The times are simulated.
32 devices in a mesh: gx: 4 (over x, core), gy: 8 (over z, y).
Axes of the slice: x: 2, y: 2, z: 4, core: 2. Of those that a mesh axis runs over, the one named last changes fastest.
Arguments:
- electric: float32 [3, 64, 128, 256], P(None, 'gx', 'gy'), may hold values from -6 to 6
- magnetic: float32 [3, 64, 128, 256], P(None, 'gx', 'gy'), may hold values from -6 to 6
- aux_electric: float32 [6, 64, 128, 256], P(None, 'gx', 'gy'), may hold values from -3 to 3
- aux_magnetic: float32 [6, 64, 128, 256], P(None, 'gx', 'gy'), may hold values from -3 to 3
- grades: int32 [3, 64, 128, 256], P(None, 'gx', 'gy'), may hold values from 0 to 3
- permittivity: float32 [64, 128, 256], P('gx', 'gy'), may hold values from 1 to 8
- dipole_cell: int32 [3, 16384], P(None, ('gx', 'gy')), may hold values from 0 to 255, as said below
- dipole_port: int32 [16384], P(('gx', 'gy')), may hold values from 0 to 511
- live_count: int32 [32], P(('gx', 'gy')), may hold values from 1 to 512, as said below
- injection: bfloat16 [16384, 512], P(('gx', 'gy')), may hold values from -0.25 to 0.25
- waveform: bfloat16 [512, 16], replicated, may hold values from -6 to 6
Outputs:
- electric_out: float32 [3, 64, 128, 256], P(None, 'gx', 'gy')
- magnetic_out: float32 [3, 64, 128, 256], P(None, 'gx', 'gy')
- port_power: float32 [16, 512], replicated
Inputs may be any that keep to these rules, and one draw needn't show every extreme that they name: `dipole_cell`: slot s lies in the block of cells held by the device that holds slot s. The live slots of a device are its first live_count ones; some device has all 512 live.
All inputs are finite; a program needn't handle non-finite values.
Results may differ from a plain program's by a relative error of at most 0.0003.
Values sent between devices are 32-bit elements; how exact they have to be, the bound alone decides.
No kernel may reach another device: no remote copies, remote signals or barrier semaphores. Data moves between devices by JAX's collectives and lax.ppermute only.
A program may use at most 128 MiB of HBM per device.

v0:
```python
import jax
import jax.numpy as jnp
from jax import lax
from jax.sharding import PartitionSpec as P

courant = 0.55
absorb_keep = (0.0, 0.92, 0.75, 0.45)
absorb_take = (0.0, -0.06, -0.18, -0.35)
derivative_pairs = ((2, 1), (1, 2), (0, 2), (2, 0), (1, 0), (0, 1))


def passed_along(block, axis, distance):
    devices = range(lax.axis_size(axis))
    route = [(i - distance, i) for i in devices if i - distance in devices]
    return lax.ppermute(block, axis, route)


def difference(values, axis, plane, forward):
    length = values.shape[axis]
    if plane is None:
        shape = list(values.shape)
        shape[axis] = 1
        plane = jnp.zeros(shape, values.dtype)
    if forward:
        after = jnp.concatenate([lax.slice_in_dim(values, 1, length, axis=axis), plane], axis)
        return after - values
    before = jnp.concatenate([plane, lax.slice_in_dim(values, 0, length - 1, axis=axis)], axis)
    return values - before


def grade_table(grades, table):
    result = jnp.zeros(grades.shape, jnp.float32)
    for level in range(1, 4):
        result = result + jnp.where(grades == level, table[level], 0.0)
    return result


def curl_parts(field, auxiliary, keep, take, planes, forward):
    terms = []
    updated = []
    for number, (component, axis) in enumerate(derivative_pairs):
        plane = None
        if planes is not None and axis == 0:
            plane = planes[0][component - 1]
        if planes is not None and axis == 1:
            plane = planes[1][component // 2]
        slope = difference(field[component], axis, plane, forward)
        carried = keep[axis] * auxiliary[number] + take[axis] * slope
        terms.append(slope + carried)
        updated.append(carried)
    rotation = (terms[0] - terms[1], terms[2] - terms[3], terms[4] - terms[5])
    return (rotation, tuple(updated))


def inject(z_plane, current_now, cell_table, depth_table):
    weighted = cell_table * current_now[:, None]
    source = lax.dot_general(
        weighted, depth_table, (((0,), (0,)), ((), ())), precision=lax.Precision.HIGHEST
    )
    return z_plane - courant * source.reshape(z_plane.shape)


def read_cells(z_plane, cell_table, depth_table):
    rows = z_plane.reshape(cell_table.shape[1], depth_table.shape[1])
    picked = jnp.dot(cell_table, rows, precision=lax.Precision.HIGHEST)
    return jnp.sum(picked * depth_table, axis=1)


def note_power(record, drive, index):
    return lax.dynamic_update_slice_in_dim(record, drive[None, :], index, 0)


def local(
    electric,
    magnetic,
    aux_electric,
    aux_magnetic,
    grades,
    permittivity,
    dipole_cell,
    dipole_port,
    live_count,
    injection,
    waveform,
):
    depth_x, depth_y, depth_z = electric.shape[1:]
    slots = dipole_cell.shape[1]
    ports, steps = waveform.shape
    row_index = lax.axis_index("gx")
    col_index = lax.axis_index("gy")
    plane_cell = (dipole_cell[0] - row_index * depth_x) * depth_y + (
        dipole_cell[1] - col_index * depth_y
    )
    cell_table = (
        plane_cell[:, None] == jnp.arange(depth_x * depth_y, dtype=jnp.int32)[None, :]
    ).astype(jnp.float32)
    depth_table = (dipole_cell[2][:, None] == jnp.arange(depth_z, dtype=jnp.int32)[None, :]).astype(
        jnp.float32
    )
    live = (jnp.arange(slots, dtype=jnp.int32) < live_count[0]).astype(jnp.float32)
    current = jnp.dot(injection, waveform, preferred_element_type=jnp.float32) * live[:, None]
    members = (dipole_port[:, None] == jnp.arange(ports, dtype=jnp.int32)[None, :]).astype(
        jnp.float32
    )
    factor = courant / permittivity
    keep = grade_table(grades, absorb_keep)
    take = grade_table(grades, absorb_take)
    record = jnp.zeros((steps, slots), jnp.float32)

    def turn_parts(step, carry):
        field_e, field_h, memory_e, memory_h, record = carry
        next_x = passed_along(jnp.stack([field_e[1][0:1], field_e[2][0:1]]), "gx", -1)
        next_y = passed_along(jnp.stack([field_e[0][:, 0:1], field_e[2][:, 0:1]]), "gy", -1)
        rotation, memory_e = curl_parts(field_e, memory_e, keep, take, (next_x, next_y), True)
        field_h = tuple((field_h[number] - courant * rotation[number] for number in range(3)))
        prior_x = passed_along(jnp.stack([field_h[1][-1:], field_h[2][-1:]]), "gx", 1)
        prior_y = passed_along(jnp.stack([field_h[0][:, -1:], field_h[2][:, -1:]]), "gy", 1)
        rotation, memory_h = curl_parts(field_h, memory_h, keep, take, (prior_x, prior_y), False)
        current_now = lax.dynamic_slice_in_dim(current, step, 1, 1)[:, 0]
        z_plane = inject(field_e[2] + factor * rotation[2], current_now, cell_table, depth_table)
        field_e = (field_e[0] + factor * rotation[0], field_e[1] + factor * rotation[1], z_plane)
        drive = current_now * read_cells(z_plane, cell_table, depth_table)
        record = note_power(record, drive, step)
        return (field_e, field_h, memory_e, memory_h, record)

    start_state = (
        tuple((electric[number] for number in range(3))),
        tuple((magnetic[number] for number in range(3))),
        tuple((aux_electric[number] for number in range(6))),
        tuple((aux_magnetic[number] for number in range(6))),
        record,
    )
    parts_e, parts_h, parts_me, parts_mh, record = lax.fori_loop(0, steps, turn_parts, start_state)
    electric = jnp.stack(parts_e)
    magnetic = jnp.stack(parts_h)
    partial_value = jnp.dot(record, members, precision=lax.Precision.HIGHEST)
    port_power = lax.psum(partial_value, ("gx", "gy"))
    return (electric, magnetic, port_power)


def solution(mesh):
    in_specs = (
        P(None, "gx", "gy", None),
        P(None, "gx", "gy", None),
        P(None, "gx", "gy", None),
        P(None, "gx", "gy", None),
        P(None, "gx", "gy", None),
        P("gx", "gy", None),
        P(None, ("gx", "gy")),
        P(("gx", "gy")),
        P(("gx", "gy")),
        P(("gx", "gy"), None),
        P(),
    )
    out_specs = (P(None, "gx", "gy", None), P(None, "gx", "gy", None), P())
    return jax.shard_map(local, mesh=mesh, in_specs=in_specs, out_specs=out_specs, check_vma=False)
```

profile of v0, /device:TPU:0, one launch (start us, length us, event | category | flops | bytes accessed | tf_op | source)
XLA Modules:
  0.0 605.0 jit_solution(2541762445763992828)
XLA Ops:
  10.5 545.4 %while.50 = (s32[]{:T(128)}, f32[16,16,256]{2,1,0:T(8,128)S(1)}, f32[16,16,256]{2,1,0:T(8,128)S(1)}, f32[16,16,256]{2,1,0:T(8,128)S(1)}, f32[16,16,256]{2,1,0:T(...) while((s32[]{:T(128)}, f32[16,16,256]{2,1,0:T(8,128)S(1)}, ...), condition=%wide.region_2.3_spmd.clone, body=%wide.region_0.2_spmd.clone.sunk | while | flops 812285952 | bytes 56044672 | solution.py:133
  23.5 5.5 collective-permute-start.2
  55.6 5.4 collective-permute-start.2
  88.7 5.2 collective-permute-start.2
  95.8 5.3 collective-permute-start.3
  123.0 5.2 collective-permute-start.2
  130.1 5.3 collective-permute-start.3
  157.3 5.2 collective-permute-start.2
  164.4 5.3 collective-permute-start.3
  191.6 5.2 collective-permute-start.2
  198.7 5.3 collective-permute-start.3
  225.9 5.2 collective-permute-start.2
  233.0 5.3 collective-permute-start.3
  260.2 5.2 collective-permute-start.2
  267.3 5.3 collective-permute-start.3
  294.5 5.2 collective-permute-start.2
  301.6 5.3 collective-permute-start.3
  328.8 5.2 collective-permute-start.2
  335.9 5.3 collective-permute-start.3
  363.1 5.2 collective-permute-start.2
  370.2 5.3 collective-permute-start.3
  397.4 5.2 collective-permute-start.2
  404.5 5.3 collective-permute-start.3
  431.7 5.2 collective-permute-start.2
  438.8 5.3 collective-permute-start.3
  466.0 5.2 collective-permute-start.2
  473.1 5.3 collective-permute-start.3
  500.3 5.2 collective-permute-start.2
  507.4 5.3 collective-permute-start.3
  534.6 5.2 collective-permute-start.2
  541.7 5.3 collective-permute-start.3
  557.2 45.9 %psum.7 = f32[16,512]{1,0:T(8,128)} all-reduce(f32[16,512]{1,0:T(8,128)S(1)} %fusion.27), channel_id=1, replica_groups=mesh['gx'=4,'gy'=8] {'gx','gy'}, use_global_device_ids=true, to_apply=%region_3.4 | all-reduce | flops 8192 | bytes 65536 | tf_op jit(solution)/shard_map/psum | solution.py:137
  (1486 shorter events, 392.8 us)
Async XLA Ops:
  10.6 9.9 %collective-permute-start.1 = (f32[2,16,1,256]{3,2,1,0:T(1,128)S(1)}, f32[2,16,1,256]{3,2,1,0:T(1,128)S(1)}, u32[]{:S(2)}, u32[]{:S(2)}) collective-permute-start(f32[2,16,1,256]{3,2,1,0:T(1,128)S(1)} %pad_maximum_fusion.11), channel_id=1, source_target_pairs={{1,0},{2,1},{3,2},{4,3},{5,4},{6,5},{7,6},{9,8},{10,9},{11,10},{12... | collective-permute-start | bytes 98312 | tf_op jit(solution)/shard_map/while/body/eval_jaxpr/ppermute | solution.py:15
  23.5 10.2 %collective-permute-start.2 = (f32[2,16,1,256]{3,2,1,0:T(1,128)S(1)}, f32[2,16,1,256]{3,2,1,0:T(1,128)S(1)}, u32[]{:S(2)}, u32[]{:S(2)}) collective-permute-start(f32[2,16,1,256]{3,2,1,0:T(1,128)S(1)} %pad_maximum_fusion.12), channel_id=1, source_target_pairs={{0,1},{1,2},{2,3},{3,4},{4,5},{5,6},{6,7},{8,9},{9,10},{10,11},{11... | collective-permute-start | bytes 98312 | tf_op jit(solution)/shard_map/while/body/eval_jaxpr/ppermute | solution.py:15
  42.7 9.9 %collective-permute-start.1 = (f32[2,16,1,256]{3,2,1,0:T(1,128)S(1)}, f32[2,16,1,256]{3,2,1,0:T(1,128)S(1)}, u32[]{:S(2)}, u32[]{:S(2)}) collective-permute-start(f32[2,16,1,256]{3,2,1,0:T(1,128)S(1)} %pad_maximum_fusion.11), channel_id=1, source_target_pairs={{1,0},{2,1},{3,2},{4,3},{5,4},{6,5},{7,6},{9,8},{10,9},{11,10},{12... | collective-permute-start | bytes 98312 | tf_op jit(solution)/shard_map/while/body/eval_jaxpr/ppermute | solution.py:15
  55.6 11.2 %collective-permute-start.2 = (f32[2,16,1,256]{3,2,1,0:T(1,128)S(1)}, f32[2,16,1,256]{3,2,1,0:T(1,128)S(1)}, u32[]{:S(2)}, u32[]{:S(2)}) collective-permute-start(f32[2,16,1,256]{3,2,1,0:T(1,128)S(1)} %pad_maximum_fusion.12), channel_id=1, source_target_pairs={{0,1},{1,2},{2,3},{3,4},{4,5},{5,6},{6,7},{8,9},{9,10},{10,11},{11... | collective-permute-start | bytes 98312 | tf_op jit(solution)/shard_map/while/body/eval_jaxpr/ppermute | solution.py:15
  75.8 9.9 %collective-permute-start.1 = (f32[2,16,1,256]{3,2,1,0:T(1,128)S(1)}, f32[2,16,1,256]{3,2,1,0:T(1,128)S(1)}, u32[]{:S(2)}, u32[]{:S(2)}) collective-permute-start(f32[2,16,1,256]{3,2,1,0:T(1,128)S(1)} %pad_maximum_fusion.11), channel_id=1, source_target_pairs={{1,0},{2,1},{3,2},{4,3},{5,4},{6,5},{7,6},{9,8},{10,9},{11,10},{12... | collective-permute-start | bytes 98312 | tf_op jit(solution)/shard_map/while/body/eval_jaxpr/ppermute | solution.py:15
  88.7 12.4 %collective-permute-start.2 = (f32[2,16,1,256]{3,2,1,0:T(1,128)S(1)}, f32[2,16,1,256]{3,2,1,0:T(1,128)S(1)}, u32[]{:S(2)}, u32[]{:S(2)}) collective-permute-start(f32[2,16,1,256]{3,2,1,0:T(1,128)S(1)} %pad_maximum_fusion.12), channel_id=1, source_target_pairs={{0,1},{1,2},{2,3},{3,4},{4,5},{5,6},{6,7},{8,9},{9,10},{10,11},{11... | collective-permute-start | bytes 98312 | tf_op jit(solution)/shard_map/while/body/eval_jaxpr/ppermute | solution.py:15
  110.1 9.9 %collective-permute-start.1 = (f32[2,16,1,256]{3,2,1,0:T(1,128)S(1)}, f32[2,16,1,256]{3,2,1,0:T(1,128)S(1)}, u32[]{:S(2)}, u32[]{:S(2)}) collective-permute-start(f32[2,16,1,256]{3,2,1,0:T(1,128)S(1)} %pad_maximum_fusion.11), channel_id=1, source_target_pairs={{1,0},{2,1},{3,2},{4,3},{5,4},{6,5},{7,6},{9,8},{10,9},{11,10},{12... | collective-permute-start | bytes 98312 | tf_op jit(solution)/shard_map/while/body/eval_jaxpr/ppermute | solution.py:15
  123.0 12.4 %collective-permute-start.2 = (f32[2,16,1,256]{3,2,1,0:T(1,128)S(1)}, f32[2,16,1,256]{3,2,1,0:T(1,128)S(1)}, u32[]{:S(2)}, u32[]{:S(2)}) collective-permute-start(f32[2,16,1,256]{3,2,1,0:T(1,128)S(1)} %pad_maximum_fusion.12), channel_id=1, source_target_pairs={{0,1},{1,2},{2,3},{3,4},{4,5},{5,6},{6,7},{8,9},{9,10},{10,11},{11... | collective-permute-start | bytes 98312 | tf_op jit(solution)/shard_map/while/body/eval_jaxpr/ppermute | solution.py:15
  144.4 9.9 %collective-permute-start.1 = (f32[2,16,1,256]{3,2,1,0:T(1,128)S(1)}, f32[2,16,1,256]{3,2,1,0:T(1,128)S(1)}, u32[]{:S(2)}, u32[]{:S(2)}) collective-permute-start(f32[2,16,1,256]{3,2,1,0:T(1,128)S(1)} %pad_maximum_fusion.11), channel_id=1, source_target_pairs={{1,0},{2,1},{3,2},{4,3},{5,4},{6,5},{7,6},{9,8},{10,9},{11,10},{12... | collective-permute-start | bytes 98312 | tf_op jit(solution)/shard_map/while/body/eval_jaxpr/ppermute | solution.py:15
  157.3 12.4 %collective-permute-start.2 = (f32[2,16,1,256]{3,2,1,0:T(1,128)S(1)}, f32[2,16,1,256]{3,2,1,0:T(1,128)S(1)}, u32[]{:S(2)}, u32[]{:S(2)}) collective-permute-start(f32[2,16,1,256]{3,2,1,0:T(1,128)S(1)} %pad_maximum_fusion.12), channel_id=1, source_target_pairs={{0,1},{1,2},{2,3},{3,4},{4,5},{5,6},{6,7},{8,9},{9,10},{10,11},{11... | collective-permute-start | bytes 98312 | tf_op jit(solution)/shard_map/while/body/eval_jaxpr/ppermute | solution.py:15
  178.7 9.9 %collective-permute-start.1 = (f32[2,16,1,256]{3,2,1,0:T(1,128)S(1)}, f32[2,16,1,256]{3,2,1,0:T(1,128)S(1)}, u32[]{:S(2)}, u32[]{:S(2)}) collective-permute-start(f32[2,16,1,256]{3,2,1,0:T(1,128)S(1)} %pad_maximum_fusion.11), channel_id=1, source_target_pairs={{1,0},{2,1},{3,2},{4,3},{5,4},{6,5},{7,6},{9,8},{10,9},{11,10},{12... | collective-permute-start | bytes 98312 | tf_op jit(solution)/shard_map/while/body/eval_jaxpr/ppermute | solution.py:15
  191.6 12.4 %collective-permute-start.2 = (f32[2,16,1,256]{3,2,1,0:T(1,128)S(1)}, f32[2,16,1,256]{3,2,1,0:T(1,128)S(1)}, u32[]{:S(2)}, u32[]{:S(2)}) collective-permute-start(f32[2,16,1,256]{3,2,1,0:T(1,128)S(1)} %pad_maximum_fusion.12), channel_id=1, source_target_pairs={{0,1},{1,2},{2,3},{3,4},{4,5},{5,6},{6,7},{8,9},{9,10},{10,11},{11... | collective-permute-start | bytes 98312 | tf_op jit(solution)/shard_map/while/body/eval_jaxpr/ppermute | solution.py:15
  213.0 9.9 %collective-permute-start.1 = (f32[2,16,1,256]{3,2,1,0:T(1,128)S(1)}, f32[2,16,1,256]{3,2,1,0:T(1,128)S(1)}, u32[]{:S(2)}, u32[]{:S(2)}) collective-permute-start(f32[2,16,1,256]{3,2,1,0:T(1,128)S(1)} %pad_maximum_fusion.11), channel_id=1, source_target_pairs={{1,0},{2,1},{3,2},{4,3},{5,4},{6,5},{7,6},{9,8},{10,9},{11,10},{12... | collective-permute-start | bytes 98312 | tf_op jit(solution)/shard_map/while/body/eval_jaxpr/ppermute | solution.py:15
  225.9 12.4 %collective-permute-start.2 = (f32[2,16,1,256]{3,2,1,0:T(1,128)S(1)}, f32[2,16,1,256]{3,2,1,0:T(1,128)S(1)}, u32[]{:S(2)}, u32[]{:S(2)}) collective-permute-start(f32[2,16,1,256]{3,2,1,0:T(1,128)S(1)} %pad_maximum_fusion.12), channel_id=1, source_target_pairs={{0,1},{1,2},{2,3},{3,4},{4,5},{5,6},{6,7},{8,9},{9,10},{10,11},{11... | collective-permute-start | bytes 98312 | tf_op jit(solution)/shard_map/while/body/eval_jaxpr/ppermute | solution.py:15
  247.3 9.9 %collective-permute-start.1 = (f32[2,16,1,256]{3,2,1,0:T(1,128)S(1)}, f32[2,16,1,256]{3,2,1,0:T(1,128)S(1)}, u32[]{:S(2)}, u32[]{:S(2)}) collective-permute-start(f32[2,16,1,256]{3,2,1,0:T(1,128)S(1)} %pad_maximum_fusion.11), channel_id=1, source_target_pairs={{1,0},{2,1},{3,2},{4,3},{5,4},{6,5},{7,6},{9,8},{10,9},{11,10},{12... | collective-permute-start | bytes 98312 | tf_op jit(solution)/shard_map/while/body/eval_jaxpr/ppermute | solution.py:15
  260.2 12.4 %collective-permute-start.2 = (f32[2,16,1,256]{3,2,1,0:T(1,128)S(1)}, f32[2,16,1,256]{3,2,1,0:T(1,128)S(1)}, u32[]{:S(2)}, u32[]{:S(2)}) collective-permute-start(f32[2,16,1,256]{3,2,1,0:T(1,128)S(1)} %pad_maximum_fusion.12), channel_id=1, source_target_pairs={{0,1},{1,2},{2,3},{3,4},{4,5},{5,6},{6,7},{8,9},{9,10},{10,11},{11... | collective-permute-start | bytes 98312 | tf_op jit(solution)/shard_map/while/body/eval_jaxpr/ppermute | solution.py:15
  281.6 9.9 %collective-permute-start.1 = (f32[2,16,1,256]{3,2,1,0:T(1,128)S(1)}, f32[2,16,1,256]{3,2,1,0:T(1,128)S(1)}, u32[]{:S(2)}, u32[]{:S(2)}) collective-permute-start(f32[2,16,1,256]{3,2,1,0:T(1,128)S(1)} %pad_maximum_fusion.11), channel_id=1, source_target_pairs={{1,0},{2,1},{3,2},{4,3},{5,4},{6,5},{7,6},{9,8},{10,9},{11,10},{12... | collective-permute-start | bytes 98312 | tf_op jit(solution)/shard_map/while/body/eval_jaxpr/ppermute | solution.py:15
  294.5 12.4 %collective-permute-start.2 = (f32[2,16,1,256]{3,2,1,0:T(1,128)S(1)}, f32[2,16,1,256]{3,2,1,0:T(1,128)S(1)}, u32[]{:S(2)}, u32[]{:S(2)}) collective-permute-start(f32[2,16,1,256]{3,2,1,0:T(1,128)S(1)} %pad_maximum_fusion.12), channel_id=1, source_target_pairs={{0,1},{1,2},{2,3},{3,4},{4,5},{5,6},{6,7},{8,9},{9,10},{10,11},{11... | collective-permute-start | bytes 98312 | tf_op jit(solution)/shard_map/while/body/eval_jaxpr/ppermute | solution.py:15
  315.9 9.9 %collective-permute-start.1 = (f32[2,16,1,256]{3,2,1,0:T(1,128)S(1)}, f32[2,16,1,256]{3,2,1,0:T(1,128)S(1)}, u32[]{:S(2)}, u32[]{:S(2)}) collective-permute-start(f32[2,16,1,256]{3,2,1,0:T(1,128)S(1)} %pad_maximum_fusion.11), channel_id=1, source_target_pairs={{1,0},{2,1},{3,2},{4,3},{5,4},{6,5},{7,6},{9,8},{10,9},{11,10},{12... | collective-permute-start | bytes 98312 | tf_op jit(solution)/shard_map/while/body/eval_jaxpr/ppermute | solution.py:15
  328.8 12.4 %collective-permute-start.2 = (f32[2,16,1,256]{3,2,1,0:T(1,128)S(1)}, f32[2,16,1,256]{3,2,1,0:T(1,128)S(1)}, u32[]{:S(2)}, u32[]{:S(2)}) collective-permute-start(f32[2,16,1,256]{3,2,1,0:T(1,128)S(1)} %pad_maximum_fusion.12), channel_id=1, source_target_pairs={{0,1},{1,2},{2,3},{3,4},{4,5},{5,6},{6,7},{8,9},{9,10},{10,11},{11... | collective-permute-start | bytes 98312 | tf_op jit(solution)/shard_map/while/body/eval_jaxpr/ppermute | solution.py:15
  350.2 9.9 %collective-permute-start.1 = (f32[2,16,1,256]{3,2,1,0:T(1,128)S(1)}, f32[2,16,1,256]{3,2,1,0:T(1,128)S(1)}, u32[]{:S(2)}, u32[]{:S(2)}) collective-permute-start(f32[2,16,1,256]{3,2,1,0:T(1,128)S(1)} %pad_maximum_fusion.11), channel_id=1, source_target_pairs={{1,0},{2,1},{3,2},{4,3},{5,4},{6,5},{7,6},{9,8},{10,9},{11,10},{12... | collective-permute-start | bytes 98312 | tf_op jit(solution)/shard_map/while/body/eval_jaxpr/ppermute | solution.py:15
  363.1 12.4 %collective-permute-start.2 = (f32[2,16,1,256]{3,2,1,0:T(1,128)S(1)}, f32[2,16,1,256]{3,2,1,0:T(1,128)S(1)}, u32[]{:S(2)}, u32[]{:S(2)}) collective-permute-start(f32[2,16,1,256]{3,2,1,0:T(1,128)S(1)} %pad_maximum_fusion.12), channel_id=1, source_target_pairs={{0,1},{1,2},{2,3},{3,4},{4,5},{5,6},{6,7},{8,9},{9,10},{10,11},{11... | collective-permute-start | bytes 98312 | tf_op jit(solution)/shard_map/while/body/eval_jaxpr/ppermute | solution.py:15
  384.5 9.9 %collective-permute-start.1 = (f32[2,16,1,256]{3,2,1,0:T(1,128)S(1)}, f32[2,16,1,256]{3,2,1,0:T(1,128)S(1)}, u32[]{:S(2)}, u32[]{:S(2)}) collective-permute-start(f32[2,16,1,256]{3,2,1,0:T(1,128)S(1)} %pad_maximum_fusion.11), channel_id=1, source_target_pairs={{1,0},{2,1},{3,2},{4,3},{5,4},{6,5},{7,6},{9,8},{10,9},{11,10},{12... | collective-permute-start | bytes 98312 | tf_op jit(solution)/shard_map/while/body/eval_jaxpr/ppermute | solution.py:15
  397.4 12.4 %collective-permute-start.2 = (f32[2,16,1,256]{3,2,1,0:T(1,128)S(1)}, f32[2,16,1,256]{3,2,1,0:T(1,128)S(1)}, u32[]{:S(2)}, u32[]{:S(2)}) collective-permute-start(f32[2,16,1,256]{3,2,1,0:T(1,128)S(1)} %pad_maximum_fusion.12), channel_id=1, source_target_pairs={{0,1},{1,2},{2,3},{3,4},{4,5},{5,6},{6,7},{8,9},{9,10},{10,11},{11... | collective-permute-start | bytes 98312 | tf_op jit(solution)/shard_map/while/body/eval_jaxpr/ppermute | solution.py:15
  418.8 9.9 %collective-permute-start.1 = (f32[2,16,1,256]{3,2,1,0:T(1,128)S(1)}, f32[2,16,1,256]{3,2,1,0:T(1,128)S(1)}, u32[]{:S(2)}, u32[]{:S(2)}) collective-permute-start(f32[2,16,1,256]{3,2,1,0:T(1,128)S(1)} %pad_maximum_fusion.11), channel_id=1, source_target_pairs={{1,0},{2,1},{3,2},{4,3},{5,4},{6,5},{7,6},{9,8},{10,9},{11,10},{12... | collective-permute-start | bytes 98312 | tf_op jit(solution)/shard_map/while/body/eval_jaxpr/ppermute | solution.py:15
  431.7 12.4 %collective-permute-start.2 = (f32[2,16,1,256]{3,2,1,0:T(1,128)S(1)}, f32[2,16,1,256]{3,2,1,0:T(1,128)S(1)}, u32[]{:S(2)}, u32[]{:S(2)}) collective-permute-start(f32[2,16,1,256]{3,2,1,0:T(1,128)S(1)} %pad_maximum_fusion.12), channel_id=1, source_target_pairs={{0,1},{1,2},{2,3},{3,4},{4,5},{5,6},{6,7},{8,9},{9,10},{10,11},{11... | collective-permute-start | bytes 98312 | tf_op jit(solution)/shard_map/while/body/eval_jaxpr/ppermute | solution.py:15
  453.1 9.9 %collective-permute-start.1 = (f32[2,16,1,256]{3,2,1,0:T(1,128)S(1)}, f32[2,16,1,256]{3,2,1,0:T(1,128)S(1)}, u32[]{:S(2)}, u32[]{:S(2)}) collective-permute-start(f32[2,16,1,256]{3,2,1,0:T(1,128)S(1)} %pad_maximum_fusion.11), channel_id=1, source_target_pairs={{1,0},{2,1},{3,2},{4,3},{5,4},{6,5},{7,6},{9,8},{10,9},{11,10},{12... | collective-permute-start | bytes 98312 | tf_op jit(solution)/shard_map/while/body/eval_jaxpr/ppermute | solution.py:15
  466.0 12.4 %collective-permute-start.2 = (f32[2,16,1,256]{3,2,1,0:T(1,128)S(1)}, f32[2,16,1,256]{3,2,1,0:T(1,128)S(1)}, u32[]{:S(2)}, u32[]{:S(2)}) collective-permute-start(f32[2,16,1,256]{3,2,1,0:T(1,128)S(1)} %pad_maximum_fusion.12), channel_id=1, source_target_pairs={{0,1},{1,2},{2,3},{3,4},{4,5},{5,6},{6,7},{8,9},{9,10},{10,11},{11... | collective-permute-start | bytes 98312 | tf_op jit(solution)/shard_map/while/body/eval_jaxpr/ppermute | solution.py:15
  487.4 9.9 %collective-permute-start.1 = (f32[2,16,1,256]{3,2,1,0:T(1,128)S(1)}, f32[2,16,1,256]{3,2,1,0:T(1,128)S(1)}, u32[]{:S(2)}, u32[]{:S(2)}) collective-permute-start(f32[2,16,1,256]{3,2,1,0:T(1,128)S(1)} %pad_maximum_fusion.11), channel_id=1, source_target_pairs={{1,0},{2,1},{3,2},{4,3},{5,4},{6,5},{7,6},{9,8},{10,9},{11,10},{12... | collective-permute-start | bytes 98312 | tf_op jit(solution)/shard_map/while/body/eval_jaxpr/ppermute | solution.py:15
  500.3 12.4 %collective-permute-start.2 = (f32[2,16,1,256]{3,2,1,0:T(1,128)S(1)}, f32[2,16,1,256]{3,2,1,0:T(1,128)S(1)}, u32[]{:S(2)}, u32[]{:S(2)}) collective-permute-start(f32[2,16,1,256]{3,2,1,0:T(1,128)S(1)} %pad_maximum_fusion.12), channel_id=1, source_target_pairs={{0,1},{1,2},{2,3},{3,4},{4,5},{5,6},{6,7},{8,9},{9,10},{10,11},{11... | collective-permute-start | bytes 98312 | tf_op jit(solution)/shard_map/while/body/eval_jaxpr/ppermute | solution.py:15
  521.7 9.9 %collective-permute-start.1 = (f32[2,16,1,256]{3,2,1,0:T(1,128)S(1)}, f32[2,16,1,256]{3,2,1,0:T(1,128)S(1)}, u32[]{:S(2)}, u32[]{:S(2)}) collective-permute-start(f32[2,16,1,256]{3,2,1,0:T(1,128)S(1)} %pad_maximum_fusion.11), channel_id=1, source_target_pairs={{1,0},{2,1},{3,2},{4,3},{5,4},{6,5},{7,6},{9,8},{10,9},{11,10},{12... | collective-permute-start | bytes 98312 | tf_op jit(solution)/shard_map/while/body/eval_jaxpr/ppermute | solution.py:15
  534.6 12.4 %collective-permute-start.2 = (f32[2,16,1,256]{3,2,1,0:T(1,128)S(1)}, f32[2,16,1,256]{3,2,1,0:T(1,128)S(1)}, u32[]{:S(2)}, u32[]{:S(2)}) collective-permute-start(f32[2,16,1,256]{3,2,1,0:T(1,128)S(1)} %pad_maximum_fusion.12), channel_id=1, source_target_pairs={{0,1},{1,2},{2,3},{3,4},{4,5},{5,6},{6,7},{8,9},{9,10},{10,11},{11... | collective-permute-start | bytes 98312 | tf_op jit(solution)/shard_map/while/body/eval_jaxpr/ppermute | solution.py:15
  (456 other events, 2595.5 us)
where the time goes:
time: 612 us; the launch traced here: 605 us
  starting transfers between devices  205 us (33%)
  local copies, waits for them, and re-layouts  160 us (26%)
  other arithmetic  119 us (19%)
  matrix products  52.2 us (9%)
  blocking collectives  45.9 us (8%)
  waiting for transfers between devices  13.2 us (2%)
  loops' own time  7.44 us (1%)
    ppermute x64, starting transfers between devices, passed_along(): return lax.ppermute(block, axis, route)  205 us
    slice x96, local copies, waits for them, and re-layouts, difference(): lax.slice_in_dim(values, 1, length, axis=axis)  73.3 us
    sub x48, other arithmetic, turn_parts(): field_h[number] - courant * rotation[number]  50.2 us
    psum x1, blocking collectives, local(): port_power = lax.psum(partial_value, ('gx', 'gy'))  45.9 us
    add x16, other arithmetic, turn_parts(): field_e[1] + factor * rotation[1]  38.7 us
    while x832, local copies, waits for them, and re-layouts  36.9 us
    dot_general x16, matrix products, inject(): lax.dot_general(weighted, depth_table, (((0,), (0,)), ((), ())), precisio...  30.5 us
    dynamic_update_slice x16, local copies, waits for them, and re-layouts, note_power(): return lax.dynamic_update_slice_in_dim(record, drive[None, :], index, 0)  21.4 us
  transfers between devices with their start and end apart: 64, of which 16 were waited for; matrix products, arithmetic and copies ran while one was open for 22% of the time, Pallas kernels for 0%

commit v1 on v0

--- a/solution.py
+++ b/solution.py
@@ -1,3 +1,4 @@
+import functools
 import jax
 import jax.numpy as jnp
 from jax import lax
@@ -7,6 +8,14 @@
 absorb_keep = (0.0, 0.92, 0.75, 0.45)
 absorb_take = (0.0, -0.06, -0.18, -0.35)
 derivative_pairs = ((2, 1), (1, 2), (0, 2), (2, 0), (1, 0), (0, 1))
+
+
+def return_all_heaps(vector, axis_tag, net_axis):
+    front = lax.psum(lax.psum(vector, axis_name=axis_tag), axis_name=net_axis)
+    return front
+
+
+close_ratios_in = functools.partial(return_all_heaps, axis_tag="gx", net_axis="gy")
 
 
 def passed_along(block, axis, distance):
@@ -134,7 +143,7 @@
     electric = jnp.stack(parts_e)
     magnetic = jnp.stack(parts_h)
     partial_value = jnp.dot(record, members, precision=lax.Precision.HIGHEST)
-    port_power = lax.psum(partial_value, ("gx", "gy"))
+    port_power = close_ratios_in(partial_value)
     return (electric, magnetic, port_power)
 
 

time: 612 us -> 616 us (level)
    psum x1 -> x2, blocking collectives: 45.9 us -> 49.6 us  [return_all_heaps(): front = lax.psum(lax.psum(vector, axis_name=axis_tag), axis_name=net_axis)]
where the time goes in v1:
time: 616 us; the launch traced here: 610 us
  starting transfers between devices  205 us (33%)
  local copies, waits for them, and re-layouts  161 us (26%)
  other arithmetic  120 us (19%)
  matrix products  52.3 us (8%)
  blocking collectives  49.6 us (8%)
  waiting for transfers between devices  13.2 us (2%)
  loops' own time  7.44 us (1%)
    ppermute x64, starting transfers between devices, passed_along(): return lax.ppermute(block, axis, route)  205 us
    slice x96, local copies, waits for them, and re-layouts, difference(): lax.slice_in_dim(values, 1, length, axis=axis)  73.8 us
    sub x48, other arithmetic, turn_parts(): field_h[number] - courant * rotation[number]  50.8 us
    psum x2, blocking collectives, return_all_heaps(): front = lax.psum(lax.psum(vector, axis_name=axis_tag), axis_name=net_axis)  49.6 us
    add x16, other arithmetic, turn_parts(): field_e[1] + factor * rotation[1]  39 us
    while x832, local copies, waits for them, and re-layouts  36.9 us
    dot_general x16, matrix products, inject(): lax.dot_general(weighted, depth_table, (((0,), (0,)), ((), ())), precisio...  30.6 us
    dynamic_update_slice x16, local copies, waits for them, and re-layouts, note_power(): return lax.dynamic_update_slice_in_dim(record, drive[None, :], index, 0)  21.4 us
  transfers between devices with their start and end apart: 64, of which 16 were waited for; matrix products, arithmetic and copies ran while one was open for 22% of the time, Pallas kernels for 0%

profile of v1, /device:TPU:0, one launch (start us, length us, event | category | flops | bytes accessed | tf_op | source)
XLA Modules:
  0.0 609.9 jit_solution(16773848233371251133)
XLA Ops:
  10.6 546.5 %while.50 = (s32[]{:T(128)}, f32[16,16,256]{2,1,0:T(8,128)S(1)}, f32[16,16,256]{2,1,0:T(8,128)S(1)}, f32[16,16,256]{2,1,0:T(8,128)S(1)}, f32[16,16,256]{2,1,0:T(...) while((s32[]{:T(128)}, f32[16,16,256]{2,1,0:T(8,128)S(1)}, ...), condition=%wide.region_2.3_spmd.clone, body=%wide.region_0.2_spmd.clone.sunk | while | flops 812285952 | bytes 56044672 | solution.py:142
  23.6 5.5 collective-permute-start.2
  55.8 5.5 collective-permute-start.2
  89.0 5.2 collective-permute-start.2
  96.0 5.3 collective-permute-start.3
  123.4 5.2 collective-permute-start.2
  130.4 5.3 collective-permute-start.3
  157.7 5.2 collective-permute-start.2
  164.8 5.3 collective-permute-start.3
  192.1 5.2 collective-permute-start.2
  199.2 5.3 collective-permute-start.3
  226.5 5.2 collective-permute-start.2
  233.5 5.3 collective-permute-start.3
  267.9 5.3 collective-permute-start.3
  295.2 5.2 collective-permute-start.2
  302.3 5.3 collective-permute-start.3
  329.6 5.2 collective-permute-start.2
  336.6 5.3 collective-permute-start.3
  364.0 5.2 collective-permute-start.2
  371.0 5.3 collective-permute-start.3
  398.3 5.2 collective-permute-start.2
  405.4 5.3 collective-permute-start.3
  432.7 5.2 collective-permute-start.2
  439.7 5.3 collective-permute-start.3
  467.1 5.2 collective-permute-start.2
  474.1 5.3 collective-permute-start.3
  501.4 5.2 collective-permute-start.2
  508.5 5.3 collective-permute-start.3
  535.8 5.2 collective-permute-start.2
  542.9 5.3 collective-permute-start.3
  558.4 13.0 %psum.14 = f32[16,512]{1,0:T(8,128)S(1)} all-reduce(f32[16,512]{1,0:T(8,128)S(1)} %fusion.27), channel_id=1, replica_groups=mesh['gx'=4,'gy'=8] {'gx'}, use_global_device_ids=true, to_apply=%region_3.4 | all-reduce | flops 8192 | bytes 65536 | tf_op jit(solution)/shard_map/psum | solution.py:14
  571.4 36.6 %psum.15 = f32[16,512]{1,0:T(8,128)} all-reduce(f32[16,512]{1,0:T(8,128)S(1)} %psum.14), channel_id=1, replica_groups=mesh['gx'=4,'gy'=8] {'gy'}, use_global_device_ids=true, to_apply=%region_4.5 | all-reduce | flops 8192 | bytes 65536 | tf_op jit(solution)/shard_map/psum | solution.py:14
  (1487 shorter events, 399.1 us)
Async XLA Ops:
  10.7 9.9 %collective-permute-start.1 = (f32[2,16,1,256]{3,2,1,0:T(1,128)S(1)}, f32[2,16,1,256]{3,2,1,0:T(1,128)S(1)}, u32[]{:S(2)}, u32[]{:S(2)}) collective-permute-start(f32[2,16,1,256]{3,2,1,0:T(1,128)S(1)} %pad_maximum_fusion.11), channel_id=1, source_target_pairs={{1,0},{2,1},{3,2},{4,3},{5,4},{6,5},{7,6},{9,8},{10,9},{11,10},{12... | collective-permute-start | bytes 98312 | tf_op jit(solution)/shard_map/while/body/eval_jaxpr/ppermute | solution.py:24
  23.6 10.2 %collective-permute-start.2 = (f32[2,16,1,256]{3,2,1,0:T(1,128)S(1)}, f32[2,16,1,256]{3,2,1,0:T(1,128)S(1)}, u32[]{:S(2)}, u32[]{:S(2)}) collective-permute-start(f32[2,16,1,256]{3,2,1,0:T(1,128)S(1)} %pad_maximum_fusion.12), channel_id=1, source_target_pairs={{0,1},{1,2},{2,3},{3,4},{4,5},{5,6},{6,7},{8,9},{9,10},{10,11},{11... | collective-permute-start | bytes 98312 | tf_op jit(solution)/shard_map/while/body/eval_jaxpr/ppermute | solution.py:24
  42.9 9.9 %collective-permute-start.1 = (f32[2,16,1,256]{3,2,1,0:T(1,128)S(1)}, f32[2,16,1,256]{3,2,1,0:T(1,128)S(1)}, u32[]{:S(2)}, u32[]{:S(2)}) collective-permute-start(f32[2,16,1,256]{3,2,1,0:T(1,128)S(1)} %pad_maximum_fusion.11), channel_id=1, source_target_pairs={{1,0},{2,1},{3,2},{4,3},{5,4},{6,5},{7,6},{9,8},{10,9},{11,10},{12... | collective-permute-start | bytes 98312 | tf_op jit(solution)/shard_map/while/body/eval_jaxpr/ppermute | solution.py:24
  55.8 11.1 %collective-permute-start.2 = (f32[2,16,1,256]{3,2,1,0:T(1,128)S(1)}, f32[2,16,1,256]{3,2,1,0:T(1,128)S(1)}, u32[]{:S(2)}, u32[]{:S(2)}) collective-permute-start(f32[2,16,1,256]{3,2,1,0:T(1,128)S(1)} %pad_maximum_fusion.12), channel_id=1, source_target_pairs={{0,1},{1,2},{2,3},{3,4},{4,5},{5,6},{6,7},{8,9},{9,10},{10,11},{11... | collective-permute-start | bytes 98312 | tf_op jit(solution)/shard_map/while/body/eval_jaxpr/ppermute | solution.py:24
  76.0 9.9 %collective-permute-start.1 = (f32[2,16,1,256]{3,2,1,0:T(1,128)S(1)}, f32[2,16,1,256]{3,2,1,0:T(1,128)S(1)}, u32[]{:S(2)}, u32[]{:S(2)}) collective-permute-start(f32[2,16,1,256]{3,2,1,0:T(1,128)S(1)} %pad_maximum_fusion.11), channel_id=1, source_target_pairs={{1,0},{2,1},{3,2},{4,3},{5,4},{6,5},{7,6},{9,8},{10,9},{11,10},{12... | collective-permute-start | bytes 98312 | tf_op jit(solution)/shard_map/while/body/eval_jaxpr/ppermute | solution.py:24
  89.0 12.4 %collective-permute-start.2 = (f32[2,16,1,256]{3,2,1,0:T(1,128)S(1)}, f32[2,16,1,256]{3,2,1,0:T(1,128)S(1)}, u32[]{:S(2)}, u32[]{:S(2)}) collective-permute-start(f32[2,16,1,256]{3,2,1,0:T(1,128)S(1)} %pad_maximum_fusion.12), channel_id=1, source_target_pairs={{0,1},{1,2},{2,3},{3,4},{4,5},{5,6},{6,7},{8,9},{9,10},{10,11},{11... | collective-permute-start | bytes 98312 | tf_op jit(solution)/shard_map/while/body/eval_jaxpr/ppermute | solution.py:24
  110.4 9.9 %collective-permute-start.1 = (f32[2,16,1,256]{3,2,1,0:T(1,128)S(1)}, f32[2,16,1,256]{3,2,1,0:T(1,128)S(1)}, u32[]{:S(2)}, u32[]{:S(2)}) collective-permute-start(f32[2,16,1,256]{3,2,1,0:T(1,128)S(1)} %pad_maximum_fusion.11), channel_id=1, source_target_pairs={{1,0},{2,1},{3,2},{4,3},{5,4},{6,5},{7,6},{9,8},{10,9},{11,10},{12... | collective-permute-start | bytes 98312 | tf_op jit(solution)/shard_map/while/body/eval_jaxpr/ppermute | solution.py:24
  123.4 12.3 %collective-permute-start.2 = (f32[2,16,1,256]{3,2,1,0:T(1,128)S(1)}, f32[2,16,1,256]{3,2,1,0:T(1,128)S(1)}, u32[]{:S(2)}, u32[]{:S(2)}) collective-permute-start(f32[2,16,1,256]{3,2,1,0:T(1,128)S(1)} %pad_maximum_fusion.12), channel_id=1, source_target_pairs={{0,1},{1,2},{2,3},{3,4},{4,5},{5,6},{6,7},{8,9},{9,10},{10,11},{11... | collective-permute-start | bytes 98312 | tf_op jit(solution)/shard_map/while/body/eval_jaxpr/ppermute | solution.py:24
  144.8 9.9 %collective-permute-start.1 = (f32[2,16,1,256]{3,2,1,0:T(1,128)S(1)}, f32[2,16,1,256]{3,2,1,0:T(1,128)S(1)}, u32[]{:S(2)}, u32[]{:S(2)}) collective-permute-start(f32[2,16,1,256]{3,2,1,0:T(1,128)S(1)} %pad_maximum_fusion.11), channel_id=1, source_target_pairs={{1,0},{2,1},{3,2},{4,3},{5,4},{6,5},{7,6},{9,8},{10,9},{11,10},{12... | collective-permute-start | bytes 98312 | tf_op jit(solution)/shard_map/while/body/eval_jaxpr/ppermute | solution.py:24
  157.7 12.4 %collective-permute-start.2 = (f32[2,16,1,256]{3,2,1,0:T(1,128)S(1)}, f32[2,16,1,256]{3,2,1,0:T(1,128)S(1)}, u32[]{:S(2)}, u32[]{:S(2)}) collective-permute-start(f32[2,16,1,256]{3,2,1,0:T(1,128)S(1)} %pad_maximum_fusion.12), channel_id=1, source_target_pairs={{0,1},{1,2},{2,3},{3,4},{4,5},{5,6},{6,7},{8,9},{9,10},{10,11},{11... | collective-permute-start | bytes 98312 | tf_op jit(solution)/shard_map/while/body/eval_jaxpr/ppermute | solution.py:24
  179.1 9.9 %collective-permute-start.1 = (f32[2,16,1,256]{3,2,1,0:T(1,128)S(1)}, f32[2,16,1,256]{3,2,1,0:T(1,128)S(1)}, u32[]{:S(2)}, u32[]{:S(2)}) collective-permute-start(f32[2,16,1,256]{3,2,1,0:T(1,128)S(1)} %pad_maximum_fusion.11), channel_id=1, source_target_pairs={{1,0},{2,1},{3,2},{4,3},{5,4},{6,5},{7,6},{9,8},{10,9},{11,10},{12... | collective-permute-start | bytes 98312 | tf_op jit(solution)/shard_map/while/body/eval_jaxpr/ppermute | solution.py:24
  192.1 12.3 %collective-permute-start.2 = (f32[2,16,1,256]{3,2,1,0:T(1,128)S(1)}, f32[2,16,1,256]{3,2,1,0:T(1,128)S(1)}, u32[]{:S(2)}, u32[]{:S(2)}) collective-permute-start(f32[2,16,1,256]{3,2,1,0:T(1,128)S(1)} %pad_maximum_fusion.12), channel_id=1, source_target_pairs={{0,1},{1,2},{2,3},{3,4},{4,5},{5,6},{6,7},{8,9},{9,10},{10,11},{11... | collective-permute-start | bytes 98312 | tf_op jit(solution)/shard_map/while/body/eval_jaxpr/ppermute | solution.py:24
  213.5 9.9 %collective-permute-start.1 = (f32[2,16,1,256]{3,2,1,0:T(1,128)S(1)}, f32[2,16,1,256]{3,2,1,0:T(1,128)S(1)}, u32[]{:S(2)}, u32[]{:S(2)}) collective-permute-start(f32[2,16,1,256]{3,2,1,0:T(1,128)S(1)} %pad_maximum_fusion.11), channel_id=1, source_target_pairs={{1,0},{2,1},{3,2},{4,3},{5,4},{6,5},{7,6},{9,8},{10,9},{11,10},{12... | collective-permute-start | bytes 98312 | tf_op jit(solution)/shard_map/while/body/eval_jaxpr/ppermute | solution.py:24
  226.5 12.4 %collective-permute-start.2 = (f32[2,16,1,256]{3,2,1,0:T(1,128)S(1)}, f32[2,16,1,256]{3,2,1,0:T(1,128)S(1)}, u32[]{:S(2)}, u32[]{:S(2)}) collective-permute-start(f32[2,16,1,256]{3,2,1,0:T(1,128)S(1)} %pad_maximum_fusion.12), channel_id=1, source_target_pairs={{0,1},{1,2},{2,3},{3,4},{4,5},{5,6},{6,7},{8,9},{9,10},{10,11},{11... | collective-permute-start | bytes 98312 | tf_op jit(solution)/shard_map/while/body/eval_jaxpr/ppermute | solution.py:24
  247.9 9.9 %collective-permute-start.1 = (f32[2,16,1,256]{3,2,1,0:T(1,128)S(1)}, f32[2,16,1,256]{3,2,1,0:T(1,128)S(1)}, u32[]{:S(2)}, u32[]{:S(2)}) collective-permute-start(f32[2,16,1,256]{3,2,1,0:T(1,128)S(1)} %pad_maximum_fusion.11), channel_id=1, source_target_pairs={{1,0},{2,1},{3,2},{4,3},{5,4},{6,5},{7,6},{9,8},{10,9},{11,10},{12... | collective-permute-start | bytes 98312 | tf_op jit(solution)/shard_map/while/body/eval_jaxpr/ppermute | solution.py:24
  260.8 12.3 %collective-permute-start.2 = (f32[2,16,1,256]{3,2,1,0:T(1,128)S(1)}, f32[2,16,1,256]{3,2,1,0:T(1,128)S(1)}, u32[]{:S(2)}, u32[]{:S(2)}) collective-permute-start(f32[2,16,1,256]{3,2,1,0:T(1,128)S(1)} %pad_maximum_fusion.12), channel_id=1, source_target_pairs={{0,1},{1,2},{2,3},{3,4},{4,5},{5,6},{6,7},{8,9},{9,10},{10,11},{11... | collective-permute-start | bytes 98312 | tf_op jit(solution)/shard_map/while/body/eval_jaxpr/ppermute | solution.py:24
  282.2 9.9 %collective-permute-start.1 = (f32[2,16,1,256]{3,2,1,0:T(1,128)S(1)}, f32[2,16,1,256]{3,2,1,0:T(1,128)S(1)}, u32[]{:S(2)}, u32[]{:S(2)}) collective-permute-start(f32[2,16,1,256]{3,2,1,0:T(1,128)S(1)} %pad_maximum_fusion.11), channel_id=1, source_target_pairs={{1,0},{2,1},{3,2},{4,3},{5,4},{6,5},{7,6},{9,8},{10,9},{11,10},{12... | collective-permute-start | bytes 98312 | tf_op jit(solution)/shard_map/while/body/eval_jaxpr/ppermute | solution.py:24
  295.2 12.4 %collective-permute-start.2 = (f32[2,16,1,256]{3,2,1,0:T(1,128)S(1)}, f32[2,16,1,256]{3,2,1,0:T(1,128)S(1)}, u32[]{:S(2)}, u32[]{:S(2)}) collective-permute-start(f32[2,16,1,256]{3,2,1,0:T(1,128)S(1)} %pad_maximum_fusion.12), channel_id=1, source_target_pairs={{0,1},{1,2},{2,3},{3,4},{4,5},{5,6},{6,7},{8,9},{9,10},{10,11},{11... | collective-permute-start | bytes 98312 | tf_op jit(solution)/shard_map/while/body/eval_jaxpr/ppermute | solution.py:24
  316.6 9.9 %collective-permute-start.1 = (f32[2,16,1,256]{3,2,1,0:T(1,128)S(1)}, f32[2,16,1,256]{3,2,1,0:T(1,128)S(1)}, u32[]{:S(2)}, u32[]{:S(2)}) collective-permute-start(f32[2,16,1,256]{3,2,1,0:T(1,128)S(1)} %pad_maximum_fusion.11), channel_id=1, source_target_pairs={{1,0},{2,1},{3,2},{4,3},{5,4},{6,5},{7,6},{9,8},{10,9},{11,10},{12... | collective-permute-start | bytes 98312 | tf_op jit(solution)/shard_map/while/body/eval_jaxpr/ppermute | solution.py:24
  329.6 12.3 %collective-permute-start.2 = (f32[2,16,1,256]{3,2,1,0:T(1,128)S(1)}, f32[2,16,1,256]{3,2,1,0:T(1,128)S(1)}, u32[]{:S(2)}, u32[]{:S(2)}) collective-permute-start(f32[2,16,1,256]{3,2,1,0:T(1,128)S(1)} %pad_maximum_fusion.12), channel_id=1, source_target_pairs={{0,1},{1,2},{2,3},{3,4},{4,5},{5,6},{6,7},{8,9},{9,10},{10,11},{11... | collective-permute-start | bytes 98312 | tf_op jit(solution)/shard_map/while/body/eval_jaxpr/ppermute | solution.py:24
  351.0 9.9 %collective-permute-start.1 = (f32[2,16,1,256]{3,2,1,0:T(1,128)S(1)}, f32[2,16,1,256]{3,2,1,0:T(1,128)S(1)}, u32[]{:S(2)}, u32[]{:S(2)}) collective-permute-start(f32[2,16,1,256]{3,2,1,0:T(1,128)S(1)} %pad_maximum_fusion.11), channel_id=1, source_target_pairs={{1,0},{2,1},{3,2},{4,3},{5,4},{6,5},{7,6},{9,8},{10,9},{11,10},{12... | collective-permute-start | bytes 98312 | tf_op jit(solution)/shard_map/while/body/eval_jaxpr/ppermute | solution.py:24
  364.0 12.4 %collective-permute-start.2 = (f32[2,16,1,256]{3,2,1,0:T(1,128)S(1)}, f32[2,16,1,256]{3,2,1,0:T(1,128)S(1)}, u32[]{:S(2)}, u32[]{:S(2)}) collective-permute-start(f32[2,16,1,256]{3,2,1,0:T(1,128)S(1)} %pad_maximum_fusion.12), channel_id=1, source_target_pairs={{0,1},{1,2},{2,3},{3,4},{4,5},{5,6},{6,7},{8,9},{9,10},{10,11},{11... | collective-permute-start | bytes 98312 | tf_op jit(solution)/shard_map/while/body/eval_jaxpr/ppermute | solution.py:24
  385.4 9.9 %collective-permute-start.1 = (f32[2,16,1,256]{3,2,1,0:T(1,128)S(1)}, f32[2,16,1,256]{3,2,1,0:T(1,128)S(1)}, u32[]{:S(2)}, u32[]{:S(2)}) collective-permute-start(f32[2,16,1,256]{3,2,1,0:T(1,128)S(1)} %pad_maximum_fusion.11), channel_id=1, source_target_pairs={{1,0},{2,1},{3,2},{4,3},{5,4},{6,5},{7,6},{9,8},{10,9},{11,10},{12... | collective-permute-start | bytes 98312 | tf_op jit(solution)/shard_map/while/body/eval_jaxpr/ppermute | solution.py:24
  398.3 12.3 %collective-permute-start.2 = (f32[2,16,1,256]{3,2,1,0:T(1,128)S(1)}, f32[2,16,1,256]{3,2,1,0:T(1,128)S(1)}, u32[]{:S(2)}, u32[]{:S(2)}) collective-permute-start(f32[2,16,1,256]{3,2,1,0:T(1,128)S(1)} %pad_maximum_fusion.12), channel_id=1, source_target_pairs={{0,1},{1,2},{2,3},{3,4},{4,5},{5,6},{6,7},{8,9},{9,10},{10,11},{11... | collective-permute-start | bytes 98312 | tf_op jit(solution)/shard_map/while/body/eval_jaxpr/ppermute | solution.py:24
  419.7 9.9 %collective-permute-start.1 = (f32[2,16,1,256]{3,2,1,0:T(1,128)S(1)}, f32[2,16,1,256]{3,2,1,0:T(1,128)S(1)}, u32[]{:S(2)}, u32[]{:S(2)}) collective-permute-start(f32[2,16,1,256]{3,2,1,0:T(1,128)S(1)} %pad_maximum_fusion.11), channel_id=1, source_target_pairs={{1,0},{2,1},{3,2},{4,3},{5,4},{6,5},{7,6},{9,8},{10,9},{11,10},{12... | collective-permute-start | bytes 98312 | tf_op jit(solution)/shard_map/while/body/eval_jaxpr/ppermute | solution.py:24
  432.7 12.4 %collective-permute-start.2 = (f32[2,16,1,256]{3,2,1,0:T(1,128)S(1)}, f32[2,16,1,256]{3,2,1,0:T(1,128)S(1)}, u32[]{:S(2)}, u32[]{:S(2)}) collective-permute-start(f32[2,16,1,256]{3,2,1,0:T(1,128)S(1)} %pad_maximum_fusion.12), channel_id=1, source_target_pairs={{0,1},{1,2},{2,3},{3,4},{4,5},{5,6},{6,7},{8,9},{9,10},{10,11},{11... | collective-permute-start | bytes 98312 | tf_op jit(solution)/shard_map/while/body/eval_jaxpr/ppermute | solution.py:24
  454.1 9.9 %collective-permute-start.1 = (f32[2,16,1,256]{3,2,1,0:T(1,128)S(1)}, f32[2,16,1,256]{3,2,1,0:T(1,128)S(1)}, u32[]{:S(2)}, u32[]{:S(2)}) collective-permute-start(f32[2,16,1,256]{3,2,1,0:T(1,128)S(1)} %pad_maximum_fusion.11), channel_id=1, source_target_pairs={{1,0},{2,1},{3,2},{4,3},{5,4},{6,5},{7,6},{9,8},{10,9},{11,10},{12... | collective-permute-start | bytes 98312 | tf_op jit(solution)/shard_map/while/body/eval_jaxpr/ppermute | solution.py:24
  467.1 12.3 %collective-permute-start.2 = (f32[2,16,1,256]{3,2,1,0:T(1,128)S(1)}, f32[2,16,1,256]{3,2,1,0:T(1,128)S(1)}, u32[]{:S(2)}, u32[]{:S(2)}) collective-permute-start(f32[2,16,1,256]{3,2,1,0:T(1,128)S(1)} %pad_maximum_fusion.12), channel_id=1, source_target_pairs={{0,1},{1,2},{2,3},{3,4},{4,5},{5,6},{6,7},{8,9},{9,10},{10,11},{11... | collective-permute-start | bytes 98312 | tf_op jit(solution)/shard_map/while/body/eval_jaxpr/ppermute | solution.py:24
  488.5 9.9 %collective-permute-start.1 = (f32[2,16,1,256]{3,2,1,0:T(1,128)S(1)}, f32[2,16,1,256]{3,2,1,0:T(1,128)S(1)}, u32[]{:S(2)}, u32[]{:S(2)}) collective-permute-start(f32[2,16,1,256]{3,2,1,0:T(1,128)S(1)} %pad_maximum_fusion.11), channel_id=1, source_target_pairs={{1,0},{2,1},{3,2},{4,3},{5,4},{6,5},{7,6},{9,8},{10,9},{11,10},{12... | collective-permute-start | bytes 98312 | tf_op jit(solution)/shard_map/while/body/eval_jaxpr/ppermute | solution.py:24
  501.4 12.4 %collective-permute-start.2 = (f32[2,16,1,256]{3,2,1,0:T(1,128)S(1)}, f32[2,16,1,256]{3,2,1,0:T(1,128)S(1)}, u32[]{:S(2)}, u32[]{:S(2)}) collective-permute-start(f32[2,16,1,256]{3,2,1,0:T(1,128)S(1)} %pad_maximum_fusion.12), channel_id=1, source_target_pairs={{0,1},{1,2},{2,3},{3,4},{4,5},{5,6},{6,7},{8,9},{9,10},{10,11},{11... | collective-permute-start | bytes 98312 | tf_op jit(solution)/shard_map/while/body/eval_jaxpr/ppermute | solution.py:24
  522.8 9.9 %collective-permute-start.1 = (f32[2,16,1,256]{3,2,1,0:T(1,128)S(1)}, f32[2,16,1,256]{3,2,1,0:T(1,128)S(1)}, u32[]{:S(2)}, u32[]{:S(2)}) collective-permute-start(f32[2,16,1,256]{3,2,1,0:T(1,128)S(1)} %pad_maximum_fusion.11), channel_id=1, source_target_pairs={{1,0},{2,1},{3,2},{4,3},{5,4},{6,5},{7,6},{9,8},{10,9},{11,10},{12... | collective-permute-start | bytes 98312 | tf_op jit(solution)/shard_map/while/body/eval_jaxpr/ppermute | solution.py:24
  535.8 12.3 %collective-permute-start.2 = (f32[2,16,1,256]{3,2,1,0:T(1,128)S(1)}, f32[2,16,1,256]{3,2,1,0:T(1,128)S(1)}, u32[]{:S(2)}, u32[]{:S(2)}) collective-permute-start(f32[2,16,1,256]{3,2,1,0:T(1,128)S(1)} %pad_maximum_fusion.12), channel_id=1, source_target_pairs={{0,1},{1,2},{2,3},{3,4},{4,5},{5,6},{6,7},{8,9},{9,10},{10,11},{11... | collective-permute-start | bytes 98312 | tf_op jit(solution)/shard_map/while/body/eval_jaxpr/ppermute | solution.py:24
  (456 other events, 2602.8 us)
